TPU v7x, 32 devices: a whole 2x2x4 slice. The times are simulated.
32 devices in a mesh: row: 4 (over y, core), col: 8 (over z, x).
Axes of the slice: x: 2, y: 2, z: 4, core: 2. Of those that a mesh axis runs over, the one named last changes fastest.
Arguments:
- templates: float32 [96, 3, 1024], P(('row', 'col')), may hold values from -600 to 600
Outputs:
- similar: float32 [96, 96], P(('row', 'col'))
All inputs are finite; a program needn't handle non-finite values.
Results may differ from a plain program's by a relative error of at most 0.0012.
Values may be sent and summed in bfloat16 or wider, within the bound.
A program may use at most 128 MiB of HBM per device.

v0:
```python
import functools
import math

import jax
import jax.numpy as jnp
import numpy as np
from jax import lax
from jax.experimental import pallas as pl
from jax.experimental.pallas import tpu as pltpu
from jax.sharding import PartitionSpec as P

LAGS = 512
LANES = 128
SUBS = 8
CORES = 2
MESH = pl.DeviceIdType.MESH


def forward_table(samples, transform_len):
    half_len = transform_len // 2
    sample_idx = np.arange(samples)[:, None]
    slot_idx = np.arange(transform_len)[None, :]
    freq_idx = np.where(slot_idx < half_len, slot_idx, slot_idx - half_len)
    phases = sample_idx * freq_idx % transform_len
    angles = phases.astype(np.float32) * np.float32(2.0 * math.pi / transform_len)
    nyquist = np.where(sample_idx % 2 == 0, 1.0, -1.0)
    basis = np.where(
        slot_idx < half_len,
        np.cos(angles),
        np.where(slot_idx == half_len, nyquist, -np.sin(angles)),
    )
    return basis.astype(np.float32).astype(jnp.bfloat16)


def inverse_table(transform_len, lag_total):
    half_len = transform_len // 2
    slot_idx = np.arange(transform_len)[:, None]
    lag_idx = np.arange(lag_total)[None, :] - lag_total // 2
    freq_idx = np.where(slot_idx < half_len, slot_idx, slot_idx - half_len)
    phases = freq_idx * lag_idx % transform_len
    angles = phases.astype(np.float32) * np.float32(2.0 * math.pi / transform_len)
    weight = (np.where(freq_idx == 0, 1.0, 2.0) / transform_len).astype(np.float32)
    nyquist = np.where(lag_idx % 2 == 0, 1.0, -1.0) / transform_len
    basis = np.where(
        slot_idx < half_len,
        weight * np.cos(angles),
        np.where(slot_idx == half_len, nyquist, -weight * np.sin(angles)),
    )
    return basis.astype(np.float32).astype(jnp.bfloat16)


def each(count, step):
    if count <= 8:
        for k in range(count):
            step(k)
    else:
        lax.fori_loop(0, count, lambda k, carry: (step(k), carry)[1], 0)


def kernel(
    rows,
    cols,
    x_hbm,
    forward_hbm,
    inverse_hbm,
    out_ref,
    x_ref,
    stage,
    gathered,
    forward,
    inverse,
    flat,
    waves,
    own,
    spectra,
    cross,
    outgoing,
    incoming,
    send_sem,
    recv_sem,
    table_sem,
    result_sem,
):
    n, comps, samples = x_ref.shape
    chunks = samples // LANES
    lines = n * comps * chunks
    half = forward.shape[1] // 2
    tables = [
        pltpu.make_async_copy(forward_hbm, forward, table_sem.at[0]),
        pltpu.make_async_copy(inverse_hbm, inverse, table_sem.at[1]),
    ]
    tall = rows // CORES
    wide = 2 ** int(math.log2(math.sqrt(cols)))
    deep = cols // wide
    plane = tall * wide
    slots = plane * deep
    row = lax.axis_index("row")
    col = lax.axis_index("col")
    my_y, my_core = row // CORES, row % CORES
    my_z, my_x = col // wide, col % wide
    my_xy = my_y * wide + my_x

    def place(xy, z, core):
        return (xy // wide) * CORES + core, z * wide + xy % wide

    def slot_of(xy, z):
        return (xy // wide) * cols + z * wide + xy % wide

    def partner(me, count, k):
        if count & (count - 1):
            return (me + k) % count
        found, bit = 0, 1
        while bit < count:
            found, bit = found + (me // bit + k // bit) % 2 * bit, bit * 2
        return found

    def up(k):
        return partner(my_z, deep, 1 + k)

    def beside(k):
        return partner(my_xy, plane, plane - 1 - k)

    other = 1 - my_core
    mine = slot_of(my_xy, my_z)

    barrier = pltpu.get_barrier_semaphore()

    def greet(xy, z, core):
        pl.semaphore_signal(
            barrier, inc=1, device_id=place(xy, z, core), device_id_type=MESH
        )

    each(deep - 1, lambda k: greet(my_xy, up(k), my_core))
    each(plane - 1, lambda k: greet(beside(k), my_z, my_core))
    greet(my_xy, my_z, other)

    taken = pltpu.make_async_copy(x_hbm, x_ref, table_sem.at[2])
    taken.start()
    for table in tables:
        table.start()
    taken.wait()

    for t in range(n):
        x = x_ref[t]
        scale = lax.rsqrt(jnp.mean(x * x, axis=1, keepdims=True) + 1e-06) / math.sqrt(samples)
        rounded = (x * scale).astype(jnp.bfloat16).astype(jnp.float32)
        for q in range(chunks):
            stage[pl.ds(t * comps * chunks + q, comps, stride=chunks), :] = rounded[
                :, q * LANES : (q + 1) * LANES
            ]
    gathered[mine] = stage[:lines].reshape(n * comps, chunks, LANES).astype(jnp.bfloat16)
    pl.semaphore_wait(barrier, deep - 1 + plane - 1 + 1)

    def copy(slot, to, sem, landing=None):
        landing = slot if landing is None else landing
        return pltpu.make_async_remote_copy(
            src_ref=gathered.at[slot],
            dst_ref=gathered.at[landing],
            send_sem=send_sem.at[sem],
            recv_sem=recv_sem.at[landing],
            device_id=to,
            device_id_type=MESH,
        )

    def to_plane(slot, z, k):
        return copy(slot, place(beside(k), my_z, my_core), z * plane + k)

    def to_column(k):
        return copy(mine, place(my_xy, up(k), my_core), slots + k)

    def to_sibling():
        return copy(mine, place(my_xy, my_z, other), slots + deep, slots)

    def arrived(slot):
        copy(slot, place(my_xy, my_z, other), slots + deep).wait_recv()

    each(deep - 1, lambda k: to_column(deep - 2 - k).start())
    to_sibling().start()
    each(plane - 1, lambda k: to_plane(mine, my_z, k).start())

    rows_block = waves.shape[0] // comps
    block = rows_block // n
    blocks = slots // block

    def unpack(slot):
        at = pl.multiple_of(slot * lines, SUBS)
        flat[pl.ds(at, lines), :] = gathered[slot].astype(jnp.float32).reshape(lines, LANES)

    def pass_on(k):
        z = up(k)
        slot = slot_of(my_xy, z)
        arrived(slot)
        each(plane - 1, lambda m: to_plane(slot, z, m).start())

    each(deep - 1, pass_on)
    arrived(slots)
    stage[lines:] = gathered[slots].astype(jnp.float32).reshape(lines, LANES)
    tables[0].wait()
    local = jnp.concatenate(
        [stage[pl.ds(q, CORES * n * comps, stride=chunks), :] for q in range(chunks)], axis=1
    )
    pad = own.shape[1] - local.shape[0]
    local = jnp.concatenate([local, jnp.zeros((pad, samples), jnp.float32)], axis=0)
    spectrum = jnp.dot(
        local.astype(jnp.bfloat16), forward[...], preferred_element_type=jnp.float32
    )
    spectrum = spectrum.astype(jnp.bfloat16).astype(jnp.float32)
    real, imag = spectrum[:, :half], spectrum[:, half:]
    bins = lax.broadcasted_iota(jnp.int32, (1, half), 1)
    own[0] = real
    own[1] = jnp.where(bins == 0, 0.0, imag)
    own[2] = jnp.where(bins == 0, imag, real)

    tables[1].wait()
    if blocks == 1:
        for k in range(deep):
            unpack(slot_of(my_xy, k))

    def take(k):
        slot = slot_of(beside(k % (plane - 1)), partner(my_z, deep, k // (plane - 1)))
        arrived(slot)
        if blocks == 1:
            unpack(slot)

    lax.fori_loop(0, (plane - 1) * deep, lambda k, carry: (take(k), carry)[1], 0)

    stride = comps * chunks

    def result(b):
        return pltpu.make_async_remote_copy(
            src_ref=outgoing.at[b],
            dst_ref=incoming.at[b],
            send_sem=result_sem.at[b],
            recv_sem=result_sem.at[blocks + b],
            device_id=place(my_xy, my_z, other),
            device_id_type=MESH,
        )

    def compare(b):
        if blocks > 1:
            flat[...] = (
                gathered[pl.ds(b * block, block)]
                .astype(jnp.float32)
                .reshape(block * n * comps * chunks, LANES)
            )
        for c in range(comps):
            for q in range(chunks):
                waves[c * rows_block : (c + 1) * rows_block, q * LANES : (q + 1) * LANES] = flat[
                    pl.ds(c * chunks + q, rows_block, stride=stride), :
                ].astype(jnp.bfloat16)

        def multiply(core, f):
            g = half + f
            for j in range(0, rows_block, 16):
                for i in range(core * n, (core + 1) * n):
                    even, odd = 0.0, 0.0
                    for c in range(comps):
                        at = c * rows_block + j
                        real = spectra[at : at + 16, f : f + LANES]
                        imag = spectra[at : at + 16, g : g + LANES]
                        r = i * comps + c
                        plain = own[0, r : r + 1, f : f + LANES]
                        turned = own[1, r : r + 1, f : f + LANES]
                        mixed = own[2, r : r + 1, f : f + LANES]
                        even = even + (plain * real + turned * imag)
                        odd = odd + (mixed * imag - turned * real)
                    at = i * rows_block + j
                    cross[at : at + 16, f : f + LANES] = even.astype(jnp.bfloat16)
                    cross[at : at + 16, g : g + LANES] = odd.astype(jnp.bfloat16)

        for f in range(0, half, LANES):
            g = half + f
            basis = jnp.concatenate(
                [forward[:, f : f + LANES], forward[:, g : g + LANES]], axis=1
            )
            found = jnp.dot(waves[...], basis, preferred_element_type=jnp.float32)
            found = found.astype(jnp.bfloat16).astype(jnp.float32)
            spectra[:, f : f + LANES] = found[:, :LANES]
            spectra[:, g : g + LANES] = found[:, LANES:]
            multiply(1, f)

        def similar(core):
            if core == 0:
                for f in range(0, half, LANES):
                    multiply(0, f)
            first = core * n * rows_block
            lagged = jnp.dot(
                cross[first : first + n * rows_block],
                inverse[...],
                preferred_element_type=jnp.float32,
            )
            top = lagged[:, :LANES]
            for at in range(LANES, LAGS, LANES):
                top = jnp.maximum(top, lagged[:, at : at + LANES])
            flipped = jnp.max(top.T, axis=0, keepdims=True)
            return jnp.concatenate(
                [flipped[:, i * rows_block : (i + 1) * rows_block] for i in range(n)], axis=0
            )

        outgoing[b] = similar(1)
        result(b).start()
        out = similar(0)
        result(b).wait_recv()
        theirs = incoming[b]
        low = jnp.where(my_core == 0, out, theirs)
        high = jnp.where(my_core == 0, theirs, out)
        if blocks == 1:
            part = cols * n
            out_ref[...] = jnp.concatenate(
                [
                    kind[:, y * part : (y + 1) * part]
                    for y in range(tall)
                    for kind in (low, high)
                ],
                axis=1,
            )
        else:
            out_ref[b, 0] = low
            out_ref[b, 1] = high
        result(b).wait_send()

    each(blocks, compare)

    each(
        deep * (plane - 1),
        lambda k: to_plane(mine, k // (plane - 1), k % (plane - 1)).wait_send(),
    )
    each(deep - 1, lambda k: to_column(k).wait_send())
    to_sibling().wait_send()


def body(templates):
    n, comps, samples = templates.shape
    rows = lax.axis_size("row")
    cols = lax.axis_size("col")
    slots = rows * cols // CORES
    block = math.gcd(slots, 16)
    blocks = slots // block
    chunks = samples // LANES
    transform_len = samples + LAGS // 2
    forward = forward_table(samples, transform_len)
    inverse = inverse_table(transform_len, LAGS)
    vmem = pl.BlockSpec(memory_space=pltpu.VMEM)
    hbm = pl.BlockSpec(memory_space=pltpu.HBM)
    local = CORES * n * comps
    shape = (n, CORES * slots * n) if blocks == 1 else (blocks, CORES, n, block * n)
    out = pl.pallas_call(
        functools.partial(kernel, rows, cols),
        out_shape=pltpu.VMEM(shape, jnp.float32),
        in_specs=[hbm, hbm, hbm],
        out_specs=vmem,
        scratch_shapes=[
            pltpu.VMEM(templates.shape, jnp.float32),
            pltpu.VMEM((CORES * n * comps * chunks, LANES), jnp.float32),
            pltpu.VMEM((slots + 1, n * comps, chunks, LANES), jnp.bfloat16),
            pltpu.VMEM(forward.shape, jnp.bfloat16),
            pltpu.VMEM(inverse.shape, jnp.bfloat16),
            pltpu.VMEM((block * n * comps * chunks, LANES), jnp.float32),
            pltpu.VMEM((comps * block * n, samples), jnp.bfloat16),
            pltpu.VMEM((3, local + -local % 16, transform_len // 2), jnp.float32),
            pltpu.VMEM((comps * block * n, transform_len), jnp.float32),
            pltpu.VMEM((CORES * n * block * n, transform_len), jnp.bfloat16),
            pltpu.VMEM((blocks, n, block * n), jnp.float32),
            pltpu.VMEM((blocks, n, block * n), jnp.float32),
            pltpu.SemaphoreType.DMA((slots + cols + 1,)),
            pltpu.SemaphoreType.DMA((slots + 1,)),
            pltpu.SemaphoreType.DMA((3,)),
            pltpu.SemaphoreType.DMA((2 * blocks,)),
        ],
        compiler_params=pltpu.CompilerParams(collective_id=0, has_side_effects=True),
    )(templates, forward, inverse)
    if blocks == 1:
        return out
    out = out.transpose(2, 1, 0, 3).reshape(n, CORES, rows // CORES, cols * n)
    return out.transpose(0, 2, 1, 3).reshape(n, CORES * slots * n)


def solution(mesh):
    placed = (P(("row", "col"), None, None),)
    return jax.shard_map(
        body, mesh=mesh, in_specs=placed, out_specs=P(("row", "col"), None), check_vma=False
    )
```

profile of v0, /device:TPU:0, one launch (start us, length us, event | category | flops | bytes accessed | tf_op | source)
XLA Modules:
  0.0 15.5 jit_solution(11105658114739023538)
XLA Ops:
  0.0 14.9 %shard_map.37 = f32[3,96]{1,0:T(4,128)S(1)} custom-call(f32[3,3,1024]{2,1,0:T(4,128)} %x_hbm.1, bf16[1024,1280]{1,0:T(8,128)(2,1)} %constant.4.clone.forward_hbm, bf16[1280,512]{1,0:T(8,128)(2,1)} %constant.5.clone.inverse_hbm), custom_call_target="tpu_custom_call" | custom-call | tf_op jit(solution)/shard_map/pallas_call | solution.py:347
  14.9 0.6 %copy.5 = f32[3,96]{1,0:T(4,128)} copy(f32[3,96]{1,0:T(4,128)S(1)} %shard_map.37) | data formatting | bytes 2304
where the time goes:
time: 15.7 us; the launch traced here: 15.5 us
  Pallas kernels  14.9 us (95%)
  local copies, waits for them, and re-layouts  0.58 us (4%)
    pallas_call x1, Pallas kernels, body(): pl.pallas_call(functools.partial(kernel, rows, cols), out_shape=pltpu.VME...  14.9 us
    unnamed x1, local copies, waits for them, and re-layouts  0.58 us

commit v1 on v0

v1 whole, which is shorter than its diff:
```python
import functools
import math

import jax
import jax.numpy as jnp
from jax import lax
from jax.experimental import pallas as pl
from jax.experimental.pallas import tpu as pltpu
from jax.sharding import PartitionSpec as P

LAGS = 512
LANES = 128
SUBS = 8
CORES = 2
STEP = 32
SEGMENT = 40
MESH = pl.DeviceIdType.MESH


def each(count, step):
    if count <= 16:
        for k in range(count):
            step(k)
    else:
        lax.fori_loop(0, count, lambda k, carry: (step(k), carry)[1], 0)


def when(condition, step):
    pl.when(condition)(step)


def kernel(
    rows,
    cols,
    x_hbm,
    out_ref,
    x_ref,
    stage,
    gathered,
    flat,
    moved,
    waves,
    shifts,
    own_rows,
    other_rows,
    theirs,
    outbox,
    inbox,
    total,
    send_sem,
    recv_sem,
    note_send_sem,
    note_recv_sem,
    near_sem,
):
    n, comps, samples = x_ref.shape
    chunks = samples // LANES
    lines = n * comps * chunks
    tall = rows // CORES
    wide = 2 ** int(math.log2(math.sqrt(cols)))
    deep = cols // wide
    plane = tall * wide
    slots = plane * deep
    group = math.gcd(plane, 4)
    height = waves.shape[2]
    width = total.shape[1]
    blocks = LAGS // STEP
    tiles = chunks + 1
    row = lax.axis_index("row")
    col = lax.axis_index("col")
    my_y, my_core = row // CORES, row % CORES
    my_z, my_x = col // wide, col % wide
    other = 1 - my_core
    mine = my_z * plane + my_y * wide + my_x

    def where_is(slot):
        xy, z = slot % plane, slot // plane
        return xy // wide, xy % wide, z

    def place(slot, core):
        y, x, z = where_is(slot)
        return y * CORES + core, z * wide + x

    def column(slot, core):
        y, x, z = where_is(slot)
        return ((y * CORES + core) * cols + z * wide + x) * n

    by_level = sorted(range(slots), key=lambda s: (sum(where_is(s)), s))

    def chips(step):
        each(slots, lambda k: step(by_level[k] if isinstance(k, int) else k))

    barrier = pltpu.get_barrier_semaphore()

    def greet(slot, core):
        pl.semaphore_signal(barrier, inc=1, device_id=place(slot, core), device_id_type=MESH)

    chips(lambda slot: when(slot > mine, lambda: greet(slot, other)))
    greet(mine, other)

    taken = pltpu.make_async_copy(x_hbm, x_ref, near_sem.at[0])
    taken.start()
    taken.wait()

    for t in range(n):
        x = x_ref[t]
        scale = lax.rsqrt(jnp.mean(x * x, axis=1, keepdims=True) + 1e-06) / math.sqrt(samples)
        rounded = (x * scale).astype(jnp.bfloat16).astype(jnp.float32)
        for q in range(chunks):
            stage[pl.ds(t * comps * chunks + q, comps, stride=chunks), :] = rounded[
                :, q * LANES : (q + 1) * LANES
            ]
    gathered[mine] = stage[:lines].reshape(n * comps, chunks, LANES).astype(jnp.bfloat16)
    pl.semaphore_wait(barrier, mine + 1)

    def block(slot):
        return pltpu.make_async_remote_copy(
            src_ref=gathered.at[mine],
            dst_ref=gathered.at[mine],
            send_sem=send_sem.at[slot],
            recv_sem=recv_sem.at[mine],
            device_id=place(slot, other),
            device_id_type=MESH,
        )

    def arrived(slot):
        pltpu.make_async_remote_copy(
            src_ref=gathered.at[slot],
            dst_ref=gathered.at[slot],
            send_sem=send_sem.at[slot],
            recv_sem=recv_sem.at[slot],
            device_id=place(mine, other),
            device_id_type=MESH,
        ).wait_recv()

    sibling = pltpu.make_async_remote_copy(
        src_ref=gathered.at[mine],
        dst_ref=gathered.at[slots],
        send_sem=near_sem.at[1],
        recv_sem=near_sem.at[2],
        device_id=place(mine, other),
        device_id_type=MESH,
    )

    chips(lambda slot: when(slot < mine, lambda: block(slot).start()))
    sibling.start()

    def shifted_copies(half):
        local = jnp.concatenate(
            [
                stage[pl.ds(half * lines + q, n * comps, stride=chunks), :]
                for q in range(chunks)
            ]
            + [jnp.zeros((n * comps, LANES), jnp.float32)],
            axis=1,
        )
        for c in range(comps):
            parts = []
            for t in range(n):
                line = local[t * comps + c : t * comps + c + 1]
                line = jnp.broadcast_to(line, (SEGMENT, tiles * LANES))
                parts.append(pltpu.roll(line, 0, 1, stride=1, stride_axis=0))
            parts.append(jnp.zeros((LANES - n * SEGMENT, tiles * LANES), jnp.float32))
            stood = jnp.concatenate(parts, axis=0).T.astype(jnp.bfloat16)
            at = slice(half * LANES, (half + 1) * LANES)
            shifts[c * samples : (c + 1) * samples, at] = stood[:samples]
            tail = comps * samples + c * LANES
            shifts[tail : tail + LANES, at] = stood[samples:]

    own_rows[...] = jnp.zeros(own_rows.shape, jnp.float32)
    other_rows[...] = jnp.zeros(other_rows.shape, jnp.float32)
    total[...] = jnp.zeros(total.shape, jnp.float32)
    for b in range(LANES // STEP):
        for c in range(comps):
            waves[b, c, :, : 2 * LANES] = jnp.zeros((height, 2 * LANES), jnp.bfloat16)
            waves[b, c, :, (chunks + 2) * LANES :] = jnp.zeros(
                (height, 2 * LANES), jnp.bfloat16
            )
    shifted_copies(0)
    sibling.wait_recv()
    stage[lines:] = gathered[slots].astype(jnp.float32).reshape(lines, LANES)
    shifted_copies(1)

    def note(g, slot):
        return pltpu.make_async_remote_copy(
            src_ref=outbox.at[g],
            dst_ref=inbox.at[mine],
            send_sem=note_send_sem.at[slot],
            recv_sem=note_recv_sem.at[mine],
            device_id=place(slot, other),
            device_id_type=MESH,
        )

    stride = comps * chunks

    def compare(g, carry):
        first = g * group
        tops = lax.broadcasted_iota(jnp.int32, (height, width), 0)
        lane = lax.broadcasted_iota(jnp.int32, (height, width), 1)
        target = jnp.full((height, width), -1, jnp.int32)
        for k in range(group):
            slot = first + k
            core = jnp.where(slot == mine, my_core, other)
            start = jnp.where(slot >= mine, column(slot, core) - k * n, -slots * n * n)
            here = (tops >= k * n) & (tops < (k + 1) * n)
            target = jnp.where(here, start + tops, target)
        spot = lane == target

        each(group, lambda k: when(first + k > mine, lambda: arrived(first + k)))
        flat[: group * lines] = (
            gathered[pl.ds(first, group)].astype(jnp.float32).reshape(group * lines, LANES)
        )
        for c in range(comps):
            wave = jnp.concatenate(
                [flat[pl.ds(c * chunks + q, height, stride=stride), :] for q in range(chunks)]
                + [jnp.zeros((height, LANES), jnp.float32)],
                axis=1,
            )
            for b in range(LANES // STEP):
                turned = wave if b == 0 else pltpu.roll(wave, tiles * LANES - b * STEP, 1)
                turned = turned.astype(jnp.bfloat16)
                waves[b, c, :, 2 * LANES : (chunks + 2) * LANES] = turned[:, :samples]
                if b:
                    waves[b, c, :, LANES : 2 * LANES] = turned[:, samples:]

        def lined_up(c, at, size):
            parts = []
            for p in range(blocks):
                a, b = p * STEP // LANES, p % (LANES // STEP)
                start = at + a * LANES
                parts.append(waves[b, c, :, start : start + size])
            return jnp.concatenate(parts, axis=0)

        found = jnp.zeros((blocks * height, 2 * LANES), jnp.float32)
        for c in range(comps):
            for at in range(0, samples, 2 * LANES):
                base = c * samples + at
                found = found + jnp.dot(
                    lined_up(c, at, 2 * LANES),
                    shifts[base : base + 2 * LANES],
                    preferred_element_type=jnp.float32,
                )
        for c in range(comps):
            base = comps * samples + c * LANES
            found = found + jnp.dot(
                lined_up(c, samples, LANES),
                shifts[base : base + LANES],
                preferred_element_type=jnp.float32,
            )

        def part(p):
            return found[p * height : (p + 1) * height]

        low, high = part(0), part(blocks - 1)
        middle = part(1)
        for p in range(2, blocks - 1):
            middle = jnp.maximum(middle, part(p))
        ours = jnp.zeros((height, width), jnp.float32)
        place_lane = lax.broadcasted_iota(jnp.int32, (height, LANES), 1)
        note_lane = lane
        for half in range(CORES):
            at = slice(half * LANES, (half + 1) * LANES)
            mid, first_block, last_block = middle[:, at], low[:, at], high[:, at]
            core = my_core if half == 0 else other
            into = own_rows if half == 0 else other_rows
            start = column(mine, core)
            for t in range(n):
                v = place_lane - t * SEGMENT
                inside = (v >= 0) & (v < SEGMENT)
                plain = jnp.maximum(
                    jnp.where(inside, jnp.maximum(mid, first_block), -jnp.inf),
                    jnp.where((v >= 0) & (v < STEP), last_block, -jnp.inf),
                )
                turned = jnp.maximum(
                    jnp.where(inside, mid, -jnp.inf),
                    jnp.maximum(
                        jnp.where((v >= 1) & (v < SEGMENT), first_block, -jnp.inf),
                        jnp.where((v >= 0) & (v <= STEP), last_block, -jnp.inf),
                    ),
                )
                best = jnp.max(plain, axis=1, keepdims=True)
                into[t : t + 1] += jnp.sum(
                    jnp.where(spot, best, 0.0), axis=0, keepdims=True
                )
                best = jnp.max(turned, axis=1, keepdims=True)
                ours = jnp.where(note_lane == start + t, best, ours)
        outbox[g] = ours
        each(group, lambda k: when(first + k > mine, lambda: note(g, first + k).start()))
        return carry

    lax.fori_loop(mine // group, slots // group, compare, 0)

    swap = pltpu.make_async_remote_copy(
        src_ref=other_rows,
        dst_ref=theirs,
        send_sem=near_sem.at[3],
        recv_sem=near_sem.at[4],
        device_id=place(mine, other),
        device_id_type=MESH,
    )
    swap.start()

    def collect(slot):
        pltpu.make_async_remote_copy(
            src_ref=outbox.at[0],
            dst_ref=inbox.at[slot],
            send_sem=note_send_sem.at[slot],
            recv_sem=note_recv_sem.at[slot],
            device_id=place(mine, other),
            device_id_type=MESH,
        ).wait_recv()
        total[...] += inbox[slot]

    chips(lambda slot: when(slot < mine, lambda: collect(slot)))
    moved[...] = pltpu.roll(total[...], (height - mine % group * n) % height, 0)
    swap.wait_recv()
    answer = moved[:n] + own_rows[:n] + theirs[:n]
    out_ref[...] = answer[:, : out_ref.shape[1]]

    chips(lambda slot: when(slot < mine, lambda: block(slot).wait_send()))
    chips(lambda slot: when(slot > mine, lambda: note(0, slot).wait_send()))
    sibling.wait_send()
    swap.wait_send()


def body(templates):
    n, comps, samples = templates.shape
    rows = lax.axis_size("row")
    cols = lax.axis_size("col")
    slots = rows * cols // CORES
    chunks = samples // LANES
    lines = n * comps * chunks
    wide = 2 ** int(math.log2(math.sqrt(cols)))
    group = math.gcd(rows // CORES * wide, 4)
    height = group * n + -(group * n) % 16
    out_width = CORES * slots * n
    width = out_width + -out_width % LANES
    tiles = chunks + 1
    return pl.pallas_call(
        functools.partial(kernel, rows, cols),
        out_shape=pltpu.VMEM((n, out_width), jnp.float32),
        in_specs=[pl.BlockSpec(memory_space=pltpu.HBM)],
        out_specs=pl.BlockSpec(memory_space=pltpu.VMEM),
        scratch_shapes=[
            pltpu.VMEM(templates.shape, jnp.float32),
            pltpu.VMEM((CORES * lines, LANES), jnp.float32),
            pltpu.VMEM((slots + 1, n * comps, chunks, LANES), jnp.bfloat16),
            pltpu.VMEM((height * comps * chunks, LANES), jnp.float32),
            pltpu.VMEM((height, width), jnp.float32),
            pltpu.VMEM((LANES // STEP, comps, height, samples + 4 * LANES), jnp.bfloat16),
            pltpu.VMEM((comps * tiles * LANES, CORES * LANES), jnp.bfloat16),
            pltpu.VMEM((SUBS, width), jnp.float32),
            pltpu.VMEM((SUBS, width), jnp.float32),
            pltpu.VMEM((SUBS, width), jnp.float32),
            pltpu.VMEM((slots // group, height, width), jnp.float32),
            pltpu.VMEM((slots, height, width), jnp.float32),
            pltpu.VMEM((height, width), jnp.float32),
            pltpu.SemaphoreType.DMA((slots,)),
            pltpu.SemaphoreType.DMA((slots,)),
            pltpu.SemaphoreType.DMA((slots,)),
            pltpu.SemaphoreType.DMA((slots,)),
            pltpu.SemaphoreType.DMA((5,)),
        ],
        compiler_params=pltpu.CompilerParams(collective_id=0, has_side_effects=True),
    )(templates)


def solution(mesh):
    placed = (P(("row", "col"), None, None),)
    return jax.shard_map(
        body, mesh=mesh, in_specs=placed, out_specs=P(("row", "col"), None), check_vma=False
    )
```

time: 15.7 us -> 18.8 us (1.20)
  the two profiles are of different devices: /device:TPU:0 before, /device:TPU:25 now
where the time goes in v1:
time: 18.8 us; the launch traced here: 18.6 us
  Pallas kernels  18 us (96%)
  local copies, waits for them, and re-layouts  0.58 us (3%)
    pallas_call x1, Pallas kernels, body(): pl.pallas_call(functools.partial(kernel, rows, cols), out_shape=pltpu.VME...  18 us
    unnamed x1, local copies, waits for them, and re-layouts  0.58 us

profile of v1, /device:TPU:25, one launch (start us, length us, event | category | flops | bytes accessed | tf_op | source)
XLA Modules:
  0.0 18.6 jit_solution(17942463954250464403)
XLA Ops:
  0.0 18.0 %shard_map.17 = f32[3,96]{1,0:T(4,128)S(1)} custom-call(f32[3,3,1024]{2,1,0:T(4,128)} %x_hbm.1), custom_call_target="tpu_custom_call" | custom-call | tf_op jit(solution)/shard_map/pallas_call | solution.py:339
  18.1 0.6 %copy.3 = f32[3,96]{1,0:T(4,128)} copy(f32[3,96]{1,0:T(4,128)S(1)} %shard_map.17) | data formatting | bytes 2304

commit v2 on v1

v2 whole, which is shorter than its diff:
```python
import functools
import math

import jax
import jax.numpy as jnp
from jax import lax
from jax.experimental import pallas as pl
from jax.experimental.pallas import tpu as pltpu
from jax.sharding import PartitionSpec as P

LAGS = 512
LANES = 128
SUBS = 8
CORES = 2
STEP = 16
MESH = pl.DeviceIdType.MESH


def each(count, step):
    if count <= 16:
        for k in range(count):
            step(k)
    else:
        lax.fori_loop(0, count, lambda k, carry: (step(k), carry)[1], 0)


def when(condition, step):
    pl.when(condition)(step)


def kernel(
    rows,
    cols,
    x_hbm,
    out_ref,
    x_ref,
    stage,
    beside,
    column_blocks,
    lines_ref,
    flat,
    waves,
    shifts,
    answers,
    turned_rows,
    from_plane,
    from_column,
    total,
    block_sem,
    column_sem,
    plane_sem,
    answer_sem,
    turned_sem,
    from_plane_sem,
    from_column_sem,
    table_sem,
):
    n, comps, samples = x_ref.shape
    chunks = samples // LANES
    series = n * comps
    lines = series * chunks
    tall = rows // CORES
    wide = 2 ** int(math.log2(math.sqrt(cols)))
    deep = cols // wide
    plane = tall * wide
    width = total.shape[1]
    blocks = LAGS // STEP
    phases = LANES // STEP
    tiles = chunks + 1
    row = lax.axis_index("row")
    col = lax.axis_index("col")
    my_y, my_core = row // CORES, row % CORES
    my_z, my_x = col // wide, col % wide
    my_xy = my_y * wide + my_x
    other = 1 - my_core

    def place(xy, z, core):
        return (xy // wide) * CORES + core, z * wide + xy % wide

    def column(xy, z, core):
        return (((xy // wide) * CORES + core) * cols + z * wide + xy % wide) * n

    def mates(step):
        each(plane, lambda xy: when(xy != my_xy, lambda: step(xy)))

    def below(step):
        for z in range(deep - 1):
            for core in range(CORES):
                when(z < my_z, lambda: step(z, core))

    def above(step):
        for z in range(1, deep):
            for core in range(CORES):
                when(z > my_z, lambda: step(z, core))

    barrier = pltpu.get_barrier_semaphore()

    def greet(xy, z, core):
        pl.semaphore_signal(barrier, inc=1, device_id=place(xy, z, core), device_id_type=MESH)

    taken = pltpu.make_async_copy(x_hbm, x_ref, table_sem.at[0])
    taken.start()
    mates(lambda xy: greet(xy, my_z, other))
    above(lambda z, core: greet(my_xy, z, core))
    greet(my_xy, my_z, other)
    taken.wait()

    for t in range(n):
        x = x_ref[t]
        scale = lax.rsqrt(jnp.mean(x * x, axis=1, keepdims=True) + 1e-06) / math.sqrt(samples)
        rounded = (x * scale).astype(jnp.bfloat16).astype(jnp.float32)
        for q in range(chunks):
            stage[pl.ds(t * comps * chunks + q, comps, stride=chunks), :] = rounded[
                :, q * LANES : (q + 1) * LANES
            ]
    column_blocks[my_z, my_core] = (
        stage[...].reshape(series, chunks, LANES).astype(jnp.bfloat16)
    )
    pl.semaphore_wait(barrier, CORES * my_z + plane)

    mine = column_blocks.at[my_z, my_core]

    def to_column(z, core):
        return pltpu.make_async_remote_copy(
            src_ref=mine,
            dst_ref=mine,
            send_sem=block_sem.at[z * CORES + core],
            recv_sem=column_sem.at[my_z * CORES + my_core],
            device_id=place(my_xy, z, core),
            device_id_type=MESH,
        )

    def to_mate(xy):
        return pltpu.make_async_remote_copy(
            src_ref=mine,
            dst_ref=beside.at[my_xy],
            send_sem=block_sem.at[deep * CORES + xy],
            recv_sem=plane_sem.at[my_xy],
            device_id=place(xy, my_z, other),
            device_id_type=MESH,
        )

    def from_above(z, core):
        block = column_blocks.at[z, core]
        return pltpu.make_async_remote_copy(
            src_ref=block,
            dst_ref=block,
            send_sem=block_sem.at[z * CORES + core],
            recv_sem=column_sem.at[z * CORES + core],
            device_id=place(my_xy, my_z, other),
            device_id_type=MESH,
        )

    def from_mate(xy):
        return pltpu.make_async_remote_copy(
            src_ref=mine,
            dst_ref=beside.at[xy],
            send_sem=block_sem.at[deep * CORES + xy],
            recv_sem=plane_sem.at[xy],
            device_id=place(xy, my_z, other),
            device_id_type=MESH,
        )

    below(lambda z, core: to_column(z, core).start())
    mates(lambda xy: to_mate(xy).start())
    to_column(my_z, other).start()

    for m in range(phases // 2):
        for c in range(comps):
            waves[m, c, :, :LANES] = jnp.zeros((2 * SUBS, LANES), jnp.bfloat16)
            waves[m, c, :, (chunks + 2) * LANES :] = jnp.zeros(
                (2 * SUBS, 3 * LANES), jnp.bfloat16
            )
    answers[...] = jnp.zeros(answers.shape, jnp.float32)

    def settle(xy):
        when(xy != my_xy, lambda: from_mate(xy).wait_recv())
        block = beside[xy].astype(jnp.float32).reshape(lines, LANES)
        block = jnp.where(jnp.full((lines, LANES), xy) == my_xy, stage[...], block)
        lines_ref[pl.ds(pl.multiple_of(xy * lines, SUBS), lines), :] = block

    each(plane, settle)
    local = jnp.concatenate(
        [lines_ref[pl.ds(q, plane * series, stride=chunks), :] for q in range(chunks)]
        + [jnp.zeros((plane * series, LANES), jnp.float32)],
        axis=1,
    )
    segments = LANES // STEP
    for g in range(shifts.shape[1] // LANES):
        for c in range(comps):
            parts = []
            for i in range(g * segments, (g + 1) * segments):
                if i < plane * n:
                    line = local[i * comps + c : i * comps + c + 1]
                    line = jnp.broadcast_to(line, (STEP, tiles * LANES))
                    parts.append(pltpu.roll(line, 0, 1, stride=1, stride_axis=0))
                else:
                    parts.append(jnp.zeros((STEP, tiles * LANES), jnp.float32))
            stood = jnp.concatenate(parts, axis=0).T.astype(jnp.bfloat16)
            at = slice(g * LANES, (g + 1) * LANES)
            shifts[c * samples : (c + 1) * samples, at] = stood[:samples]
            tail = comps * samples + c * LANES
            shifts[tail : tail + LANES, at] = stood[samples:]

    def answer(xy):
        return pltpu.make_async_remote_copy(
            src_ref=answers.at[0, xy],
            dst_ref=from_plane.at[my_xy],
            send_sem=answer_sem.at[xy],
            recv_sem=from_plane_sem.at[my_xy],
            device_id=place(xy, my_z, other),
            device_id_type=MESH,
        )

    def give_back(z, core):
        return pltpu.make_async_remote_copy(
            src_ref=turned_rows.at[z],
            dst_ref=from_column.at[my_z, my_core],
            send_sem=turned_sem.at[z * CORES + core],
            recv_sem=from_column_sem.at[my_z * CORES + my_core],
            device_id=place(my_xy, z, core),
            device_id_type=MESH,
        )

    lane = lax.broadcasted_iota(jnp.int32, (SUBS, width), 1)
    tops = lax.broadcasted_iota(jnp.int32, (SUBS, width), 0)
    place_lane = lax.broadcasted_iota(jnp.int32, (SUBS, 2 * LANES), 1)
    seat = place_lane % STEP
    stride = comps * chunks

    def compare(k, carry):
        last = k == deep - my_z
        z = jnp.where(last, my_z, my_z + k)
        target = jnp.full((SUBS, width), -1, jnp.int32)
        for core in range(CORES):
            here = (tops >= core * n) & (tops < (core + 1) * n)
            target = jnp.where(here, column(my_xy, z, core) - core * n + tops, target)
        spot = lane == jnp.where(last, -1, target)
        spare = jnp.where(last, 1, 0)

        when(last & (my_z < deep - 1), lambda: mates(lambda xy: answer(xy).start()))
        for core in range(CORES):
            when((z > my_z) | (core != my_core), lambda: from_above(z, core).wait_recv())
        flat[: CORES * lines] = (
            column_blocks[z].astype(jnp.float32).reshape(CORES * lines, LANES)
        )
        for c in range(comps):
            wave = jnp.concatenate(
                [flat[pl.ds(c * chunks + q, SUBS, stride=stride), :] for q in range(chunks)]
                + [jnp.zeros((SUBS, LANES), jnp.float32)],
                axis=1,
            )
            for m in range(phases // 2):
                pair = [
                    wave if b == 0 else pltpu.roll(wave, tiles * LANES - b * STEP, 1)
                    for b in (2 * m, 2 * m + 1)
                ]
                pair = jnp.concatenate(pair, axis=0).astype(jnp.bfloat16)
                waves[m, c, :, 2 * LANES : (chunks + 2) * LANES] = pair[:, :samples]
                waves[m, c, :, LANES : 2 * LANES] = pair[:, samples:]

        def lined_up(c, at, size):
            parts = []
            for p in range(0, blocks + 2, 2):
                start = at + p // phases * LANES
                parts.append(waves[p % phases // 2, c, :, start : start + size])
            return jnp.concatenate(parts, axis=0)

        turned = jnp.zeros((SUBS, width), jnp.float32)
        for g in range(shifts.shape[1] // (2 * LANES)):
            at = slice(2 * g * LANES, 2 * (g + 1) * LANES)
            found = jnp.zeros(((blocks + 2) * SUBS, 2 * LANES), jnp.float32)
            for c in range(comps):
                for start in range(0, samples, 2 * LANES):
                    base = c * samples + start
                    found = found + jnp.dot(
                        lined_up(c, start, 2 * LANES),
                        shifts[base : base + 2 * LANES, at],
                        preferred_element_type=jnp.float32,
                    )
            for c in range(comps):
                base = comps * samples + c * LANES
                found = found + jnp.dot(
                    lined_up(c, samples, LANES),
                    shifts[base : base + LANES, at],
                    preferred_element_type=jnp.float32,
                )

            def part(p):
                return found[p * SUBS : (p + 1) * SUBS]

            middle = part(1)
            for p in range(2, blocks):
                middle = jnp.maximum(middle, part(p))
            plain = jnp.maximum(middle, part(0))
            swapped = jnp.maximum(middle, jnp.where(seat == 0, part(blocks), part(0)))
            for s in range(2 * segments):
                i = g * 2 * segments + s
                if i >= plane * n:
                    break
                xy, t = i // n, i % n
                part_at = slice(s // segments * LANES, (s // segments + 1) * LANES)
                v = place_lane[:, :LANES] - s % segments * STEP
                inside = (v >= 0) & (v < STEP)
                best = jnp.max(
                    jnp.where(inside, plain[:, part_at], -jnp.inf), axis=1, keepdims=True
                )
                answers[spare, xy, t : t + 1] += jnp.sum(
                    jnp.where(spot, best, 0.0), axis=0, keepdims=True
                )
                best = jnp.max(
                    jnp.where(inside, swapped[:, part_at], -jnp.inf), axis=1, keepdims=True
                )
                core = jnp.where(my_xy == xy, my_core, other)
                turned = jnp.where(lane == column(xy, my_z, core) + t, best, turned)
        turned_rows[z] = turned
        for core in range(CORES):
            when((z > my_z) | (core != my_core), lambda: give_back(z, core).start())
        return carry

    lax.fori_loop(1, deep - my_z + 1, compare, 0)

    total[...] = turned_rows[my_z]

    def collect(z, core):
        pltpu.make_async_remote_copy(
            src_ref=turned_rows.at[0],
            dst_ref=from_column.at[z, core],
            send_sem=turned_sem.at[z * CORES + core],
            recv_sem=from_column_sem.at[z * CORES + core],
            device_id=place(my_xy, my_z, other),
            device_id_type=MESH,
        ).wait_recv()
        total[...] += from_column[z, core]

    for z in range(deep):
        for core in range(CORES):
            when((z < my_z) | ((z == my_z) & (core != my_core)), lambda: collect(z, core))
    total[...] = pltpu.roll(total[...], (SUBS - my_core * n) % SUBS, 0)
    total[...] += answers[0, my_xy]

    def hear(xy):
        pltpu.make_async_remote_copy(
            src_ref=answers.at[0, xy],
            dst_ref=from_plane.at[xy],
            send_sem=answer_sem.at[xy],
            recv_sem=from_plane_sem.at[xy],
            device_id=place(xy, my_z, other),
            device_id_type=MESH,
        ).wait_recv()
        total[...] += from_plane[xy]

    when(my_z < deep - 1, lambda: mates(hear))
    out_ref[...] = total[:n, : out_ref.shape[1]]

    below(lambda z, core: to_column(z, core).wait_send())
    mates(lambda xy: to_mate(xy).wait_send())
    to_column(my_z, other).wait_send()
    when(my_z < deep - 1, lambda: mates(lambda xy: answer(xy).wait_send()))
    above(lambda z, core: give_back(z, core).wait_send())
    give_back(my_z, other).wait_send()


def body(templates):
    n, comps, samples = templates.shape
    rows = lax.axis_size("row")
    cols = lax.axis_size("col")
    chunks = samples // LANES
    series = n * comps
    lines = series * chunks
    wide = 2 ** int(math.log2(math.sqrt(cols)))
    deep = cols // wide
    plane = rows // CORES * wide
    out_width = rows * cols * n
    width = out_width + -out_width % LANES
    tiles = chunks + 1
    spread = plane * n * STEP
    spread += -spread % (2 * LANES)
    dma = pltpu.SemaphoreType.DMA
    return pl.pallas_call(
        functools.partial(kernel, rows, cols),
        out_shape=pltpu.VMEM((n, out_width), jnp.float32),
        in_specs=[pl.BlockSpec(memory_space=pltpu.HBM)],
        out_specs=pl.BlockSpec(memory_space=pltpu.VMEM),
        scratch_shapes=[
            pltpu.VMEM(templates.shape, jnp.float32),
            pltpu.VMEM((lines, LANES), jnp.float32),
            pltpu.VMEM((plane, series, chunks, LANES), jnp.bfloat16),
            pltpu.VMEM((deep, CORES, series, chunks, LANES), jnp.bfloat16),
            pltpu.VMEM((plane * lines, LANES), jnp.float32),
            pltpu.VMEM((SUBS * comps * chunks, LANES), jnp.float32),
            pltpu.VMEM(
                (LANES // STEP // 2, comps, 2 * SUBS, samples + 5 * LANES), jnp.bfloat16
            ),
            pltpu.VMEM((comps * tiles * LANES, spread), jnp.bfloat16),
            pltpu.VMEM((2, plane, SUBS, width), jnp.float32),
            pltpu.VMEM((deep, SUBS, width), jnp.float32),
            pltpu.VMEM((plane, SUBS, width), jnp.float32),
            pltpu.VMEM((deep, CORES, SUBS, width), jnp.float32),
            pltpu.VMEM((SUBS, width), jnp.float32),
            dma((deep * CORES + plane,)),
            dma((deep * CORES,)),
            dma((plane,)),
            dma((plane,)),
            dma((deep * CORES,)),
            dma((plane,)),
            dma((deep * CORES,)),
            dma((1,)),
        ],
        compiler_params=pltpu.CompilerParams(collective_id=0, has_side_effects=True),
    )(templates)


def solution(mesh):
    placed = (P(("row", "col"), None, None),)
    return jax.shard_map(
        body, mesh=mesh, in_specs=placed, out_specs=P(("row", "col"), None), check_vma=False
    )
```

time: 18.8 us -> 14.5 us (0.77)
  the two profiles are of different devices: /device:TPU:25 before, /device:TPU:0 now
where the time goes in v2:
time: 14.5 us; the launch traced here: 14.3 us
  Pallas kernels  13.8 us (95%)
  local copies, waits for them, and re-layouts  0.58 us (4%)
    pallas_call x1, Pallas kernels, body(): pl.pallas_call(functools.partial(kernel, rows, cols), out_shape=pltpu.VME...  13.8 us
    unnamed x1, local copies, waits for them, and re-layouts  0.58 us

profile of v2, /device:TPU:0, one launch (start us, length us, event | category | flops | bytes accessed | tf_op | source)
XLA Modules:
  0.0 14.3 jit_solution(4861598579116680503)
XLA Ops:
  0.0 13.8 %shard_map.17 = f32[3,96]{1,0:T(4,128)S(1)} custom-call(f32[3,3,1024]{2,1,0:T(4,128)} %x_hbm.1), custom_call_target="tpu_custom_call" | custom-call | tf_op jit(solution)/shard_map/pallas_call | solution.py:380
  13.8 0.6 %copy.3 = f32[3,96]{1,0:T(4,128)} copy(f32[3,96]{1,0:T(4,128)S(1)} %shard_map.17) | data formatting | bytes 2304

commit v3 on v2

--- a/solution.py
+++ b/solution.py
@@ -47,6 +47,7 @@
     from_column,
     total,
     block_sem,
+    column_send_sem,
     column_sem,
     plane_sem,
     answer_sem,
@@ -80,8 +81,16 @@
     def column(xy, z, core):
         return (((xy // wide) * CORES + core) * cols + z * wide + xy % wide) * n
 
+    def mate(k):
+        if plane & (plane - 1):
+            return (my_xy + k) % plane
+        found, bit = 0, 1
+        while bit < plane:
+            found, bit = found + (my_xy // bit + k // bit) % 2 * bit, bit * 2
+        return found
+
     def mates(step):
-        each(plane, lambda xy: when(xy != my_xy, lambda: step(xy)))
+        each(plane - 1, lambda k: step(mate(k + 1)))
 
     def below(step):
         for z in range(deep - 1):
@@ -110,11 +119,11 @@
         scale = lax.rsqrt(jnp.mean(x * x, axis=1, keepdims=True) + 1e-06) / math.sqrt(samples)
         rounded = (x * scale).astype(jnp.bfloat16).astype(jnp.float32)
         for q in range(chunks):
-            stage[pl.ds(t * comps * chunks + q, comps, stride=chunks), :] = rounded[
+            stage[pl.ds(t * chunks + q, comps, stride=n * chunks), :] = rounded[
                 :, q * LANES : (q + 1) * LANES
             ]
     column_blocks[my_z, my_core] = (
-        stage[...].reshape(series, chunks, LANES).astype(jnp.bfloat16)
+        stage[...].reshape(comps, n, chunks, LANES).astype(jnp.bfloat16)
     )
     pl.semaphore_wait(barrier, CORES * my_z + plane)
 
@@ -124,7 +133,7 @@
         return pltpu.make_async_remote_copy(
             src_ref=mine,
             dst_ref=mine,
-            send_sem=block_sem.at[z * CORES + core],
+            send_sem=column_send_sem.at[z * CORES + core],
             recv_sem=column_sem.at[my_z * CORES + my_core],
             device_id=place(my_xy, z, core),
             device_id_type=MESH,
@@ -134,7 +143,7 @@
         return pltpu.make_async_remote_copy(
             src_ref=mine,
             dst_ref=beside.at[my_xy],
-            send_sem=block_sem.at[deep * CORES + xy],
+            send_sem=block_sem.at[xy],
             recv_sem=plane_sem.at[my_xy],
             device_id=place(xy, my_z, other),
             device_id_type=MESH,
@@ -145,7 +154,7 @@
         return pltpu.make_async_remote_copy(
             src_ref=block,
             dst_ref=block,
-            send_sem=block_sem.at[z * CORES + core],
+            send_sem=column_send_sem.at[core],
             recv_sem=column_sem.at[z * CORES + core],
             device_id=place(my_xy, my_z, other),
             device_id_type=MESH,
@@ -155,15 +164,27 @@
         return pltpu.make_async_remote_copy(
             src_ref=mine,
             dst_ref=beside.at[xy],
-            send_sem=block_sem.at[deep * CORES + xy],
+            send_sem=block_sem.at[xy],
             recv_sem=plane_sem.at[xy],
             device_id=place(xy, my_z, other),
             device_id_type=MESH,
         )
 
-    below(lambda z, core: to_column(z, core).start())
+    def send_down(z):
+        to_column(z, my_core).start()
+        to_column(z, other).start()
+
+    when(my_z > 0, lambda: send_down(0))
     mates(lambda xy: to_mate(xy).start())
     to_column(my_z, other).start()
+    def gone(z):
+        for core in range(CORES):
+            to_column(z, core).wait_send()
+
+    def send_next(z):
+        gone(z - 1)
+        send_down(z)
+
 
     for m in range(phases // 2):
         for c in range(comps):
@@ -173,42 +194,58 @@
             )
     answers[...] = jnp.zeros(answers.shape, jnp.float32)
 
-    def settle(xy):
-        when(xy != my_xy, lambda: from_mate(xy).wait_recv())
-        block = beside[xy].astype(jnp.float32).reshape(lines, LANES)
-        block = jnp.where(jnp.full((lines, LANES), xy) == my_xy, stage[...], block)
-        lines_ref[pl.ds(pl.multiple_of(xy * lines, SUBS), lines), :] = block
-
-    each(plane, settle)
-    local = jnp.concatenate(
-        [lines_ref[pl.ds(q, plane * series, stride=chunks), :] for q in range(chunks)]
-        + [jnp.zeros((plane * series, LANES), jnp.float32)],
-        axis=1,
-    )
+    def settle(k):
+        if k == 0:
+            block = stage[...]
+        else:
+            from_mate(mate(k)).wait_recv()
+            block = beside[mate(k)].astype(jnp.float32).reshape(lines, LANES)
+        lines_ref[k * lines : (k + 1) * lines, :] = block
+
     segments = LANES // STEP
-    for g in range(shifts.shape[1] // LANES):
+    seats_of = segments // 2
+
+    def stand(g):
+        held = range(2 * g, min(2 * g + 2, plane))
+        for k in held:
+            settle(k)
+        local = jnp.concatenate(
+            [
+                lines_ref[pl.ds(2 * g * lines + q, len(held) * series, stride=chunks), :]
+                for q in range(chunks)
+            ]
+            + [jnp.zeros((len(held) * series, LANES), jnp.float32)],
+            axis=1,
+        )
         for c in range(comps):
             parts = []
-            for i in range(g * segments, (g + 1) * segments):
-                if i < plane * n:
-                    line = local[i * comps + c : i * comps + c + 1]
-                    line = jnp.broadcast_to(line, (STEP, tiles * LANES))
-                    parts.append(pltpu.roll(line, 0, 1, stride=1, stride_axis=0))
+            for s in range(segments):
+                k, t = s // seats_of, s % seats_of
+                if k < len(held) and t < n:
+                    r = k * series + c * n + t
+                    line = jnp.broadcast_to(local[r : r + 1], (STEP, tiles * LANES))
+                    line = pltpu.roll(line, 0, 1, stride=1, stride_axis=0)
                 else:
-                    parts.append(jnp.zeros((STEP, tiles * LANES), jnp.float32))
-            stood = jnp.concatenate(parts, axis=0).T.astype(jnp.bfloat16)
+                    line = jnp.zeros((STEP, tiles * LANES), jnp.float32)
+                parts.append(line.astype(jnp.bfloat16))
+            stood = jnp.concatenate(parts, axis=0).T
             at = slice(g * LANES, (g + 1) * LANES)
             shifts[c * samples : (c + 1) * samples, at] = stood[:samples]
             tail = comps * samples + c * LANES
             shifts[tail : tail + LANES, at] = stood[samples:]
 
-    def answer(xy):
-        return pltpu.make_async_remote_copy(
-            src_ref=answers.at[0, xy],
+    for z in range(1, deep - 1):
+        when(z < my_z, lambda: send_next(z))
+    for g in range((plane + 1) // 2):
+        stand(g)
+
+    def answer(k):
+        return pltpu.make_async_remote_copy(
+            src_ref=answers.at[k],
             dst_ref=from_plane.at[my_xy],
-            send_sem=answer_sem.at[xy],
+            send_sem=answer_sem.at[k],
             recv_sem=from_plane_sem.at[my_xy],
-            device_id=place(xy, my_z, other),
+            device_id=place(mate(k), my_z, other),
             device_id_type=MESH,
         )
 
@@ -226,27 +263,20 @@
     tops = lax.broadcasted_iota(jnp.int32, (SUBS, width), 0)
     place_lane = lax.broadcasted_iota(jnp.int32, (SUBS, 2 * LANES), 1)
     seat = place_lane % STEP
-    stride = comps * chunks
-
-    def compare(k, carry):
-        last = k == deep - my_z
-        z = jnp.where(last, my_z, my_z + k)
+
+    def compare(z, own):
         target = jnp.full((SUBS, width), -1, jnp.int32)
         for core in range(CORES):
             here = (tops >= core * n) & (tops < (core + 1) * n)
             target = jnp.where(here, column(my_xy, z, core) - core * n + tops, target)
-        spot = lane == jnp.where(last, -1, target)
-        spare = jnp.where(last, 1, 0)
-
-        when(last & (my_z < deep - 1), lambda: mates(lambda xy: answer(xy).start()))
-        for core in range(CORES):
-            when((z > my_z) | (core != my_core), lambda: from_above(z, core).wait_recv())
-        flat[: CORES * lines] = (
-            column_blocks[z].astype(jnp.float32).reshape(CORES * lines, LANES)
-        )
-        for c in range(comps):
+        spot = lane == target
+
+        def prepare(c):
+            flat[c, : CORES * n * chunks] = (
+                column_blocks[z, :, c].astype(jnp.float32).reshape(CORES * n * chunks, LANES)
+            )
             wave = jnp.concatenate(
-                [flat[pl.ds(c * chunks + q, SUBS, stride=stride), :] for q in range(chunks)]
+                [flat[c, pl.ds(q, SUBS, stride=chunks), :] for q in range(chunks)]
                 + [jnp.zeros((SUBS, LANES), jnp.float32)],
                 axis=1,
             )
@@ -266,8 +296,7 @@
                 parts.append(waves[p % phases // 2, c, :, start : start + size])
             return jnp.concatenate(parts, axis=0)
 
-        turned = jnp.zeros((SUBS, width), jnp.float32)
-        for g in range(shifts.shape[1] // (2 * LANES)):
+        def products(g):
             at = slice(2 * g * LANES, 2 * (g + 1) * LANES)
             found = jnp.zeros(((blocks + 2) * SUBS, 2 * LANES), jnp.float32)
             for c in range(comps):
@@ -285,6 +314,21 @@
                     shifts[base : base + LANES, at],
                     preferred_element_type=jnp.float32,
                 )
+            return found
+
+        wholes = shifts.shape[1] // (2 * LANES)
+        if own:
+            from_above(z, other).wait_recv()
+        else:
+            for core in range(CORES):
+                from_above(z, core).wait_recv()
+        for c in range(comps):
+            prepare(c)
+
+        turned = jnp.zeros((SUBS, width), jnp.float32)
+        parts = []
+        for g in range(wholes):
+            found = products(g)
 
             def part(p):
                 return found[p * SUBS : (p + 1) * SUBS]
@@ -294,31 +338,42 @@
                 middle = jnp.maximum(middle, part(p))
             plain = jnp.maximum(middle, part(0))
             swapped = jnp.maximum(middle, jnp.where(seat == 0, part(blocks), part(0)))
-            for s in range(2 * segments):
-                i = g * 2 * segments + s
-                if i >= plane * n:
+            parts.append(swapped)
+            for k, t, part_at, inside in seats(g):
+                if own:
                     break
-                xy, t = i // n, i % n
-                part_at = slice(s // segments * LANES, (s // segments + 1) * LANES)
-                v = place_lane[:, :LANES] - s % segments * STEP
-                inside = (v >= 0) & (v < STEP)
                 best = jnp.max(
                     jnp.where(inside, plain[:, part_at], -jnp.inf), axis=1, keepdims=True
                 )
-                answers[spare, xy, t : t + 1] += jnp.sum(
+                answers[k, t : t + 1] += jnp.sum(
                     jnp.where(spot, best, 0.0), axis=0, keepdims=True
                 )
+        if not own:
+            when(z == deep - 1, lambda: each(plane - 1, lambda k: answer(k + 1).start()))
+        for g in range(wholes):
+            for k, t, part_at, inside in seats(g):
                 best = jnp.max(
-                    jnp.where(inside, swapped[:, part_at], -jnp.inf), axis=1, keepdims=True
+                    jnp.where(inside, parts[g][:, part_at], -jnp.inf), axis=1, keepdims=True
                 )
-                core = jnp.where(my_xy == xy, my_core, other)
-                turned = jnp.where(lane == column(xy, my_z, core) + t, best, turned)
+                core = other if k else my_core
+                turned = jnp.where(lane == column(mate(k), my_z, core) + t, best, turned)
         turned_rows[z] = turned
         for core in range(CORES):
-            when((z > my_z) | (core != my_core), lambda: give_back(z, core).start())
-        return carry
-
-    lax.fori_loop(1, deep - my_z + 1, compare, 0)
+            if own:
+                when(core != my_core, lambda: give_back(z, core).start())
+            else:
+                give_back(z, core).start()
+
+    def seats(g):
+        for s in range(2 * segments):
+            k, t = g * 2 * segments // seats_of + s // seats_of, s % seats_of
+            if k < plane and t < n:
+                v = place_lane[:, :LANES] - s % segments * STEP
+                part_at = slice(s // segments * LANES, (s // segments + 1) * LANES)
+                yield k, t, part_at, (v >= 0) & (v < STEP)
+
+    lax.fori_loop(my_z + 1, deep, lambda z, carry: (compare(z, False), carry)[1], 0)
+    compare(my_z, True)
 
     total[...] = turned_rows[my_z]
 
@@ -337,13 +392,13 @@
         for core in range(CORES):
             when((z < my_z) | ((z == my_z) & (core != my_core)), lambda: collect(z, core))
     total[...] = pltpu.roll(total[...], (SUBS - my_core * n) % SUBS, 0)
-    total[...] += answers[0, my_xy]
+    total[...] += answers[0]
 
     def hear(xy):
         pltpu.make_async_remote_copy(
-            src_ref=answers.at[0, xy],
+            src_ref=answers.at[0],
             dst_ref=from_plane.at[xy],
-            send_sem=answer_sem.at[xy],
+            send_sem=answer_sem.at[0],
             recv_sem=from_plane_sem.at[xy],
             device_id=place(xy, my_z, other),
             device_id_type=MESH,
@@ -353,10 +408,10 @@
     when(my_z < deep - 1, lambda: mates(hear))
     out_ref[...] = total[:n, : out_ref.shape[1]]
 
-    below(lambda z, core: to_column(z, core).wait_send())
+    when(my_z > 0, lambda: gone(my_z - 1))
+    to_column(my_z, other).wait_send()
     mates(lambda xy: to_mate(xy).wait_send())
-    to_column(my_z, other).wait_send()
-    when(my_z < deep - 1, lambda: mates(lambda xy: answer(xy).wait_send()))
+    when(my_z < deep - 1, lambda: each(plane - 1, lambda k: answer(k + 1).wait_send()))
     above(lambda z, core: give_back(z, core).wait_send())
     give_back(my_z, other).wait_send()
 
@@ -374,7 +429,7 @@
     out_width = rows * cols * n
     width = out_width + -out_width % LANES
     tiles = chunks + 1
-    spread = plane * n * STEP
+    spread = plane * LANES // 2
     spread += -spread % (2 * LANES)
     dma = pltpu.SemaphoreType.DMA
     return pl.pallas_call(
@@ -385,20 +440,21 @@
         scratch_shapes=[
             pltpu.VMEM(templates.shape, jnp.float32),
             pltpu.VMEM((lines, LANES), jnp.float32),
-            pltpu.VMEM((plane, series, chunks, LANES), jnp.bfloat16),
-            pltpu.VMEM((deep, CORES, series, chunks, LANES), jnp.bfloat16),
+            pltpu.VMEM((plane, comps, n, chunks, LANES), jnp.bfloat16),
+            pltpu.VMEM((deep, CORES, comps, n, chunks, LANES), jnp.bfloat16),
             pltpu.VMEM((plane * lines, LANES), jnp.float32),
-            pltpu.VMEM((SUBS * comps * chunks, LANES), jnp.float32),
+            pltpu.VMEM((comps, SUBS * chunks, LANES), jnp.float32),
             pltpu.VMEM(
                 (LANES // STEP // 2, comps, 2 * SUBS, samples + 5 * LANES), jnp.bfloat16
             ),
             pltpu.VMEM((comps * tiles * LANES, spread), jnp.bfloat16),
-            pltpu.VMEM((2, plane, SUBS, width), jnp.float32),
+            pltpu.VMEM((plane, SUBS, width), jnp.float32),
             pltpu.VMEM((deep, SUBS, width), jnp.float32),
             pltpu.VMEM((plane, SUBS, width), jnp.float32),
             pltpu.VMEM((deep, CORES, SUBS, width), jnp.float32),
             pltpu.VMEM((SUBS, width), jnp.float32),
-            dma((deep * CORES + plane,)),
+            dma((plane,)),
+            dma((deep * CORES,)),
             dma((deep * CORES,)),
             dma((plane,)),
             dma((plane,)),

time: 14.5 us -> 14 us (0.966)
  Pallas kernels: 13.8 us -> 13.2 us
    pallas_call x1, Pallas kernels: 13.8 us -> 13.2 us  [body(): pl.pallas_call(functools.partial(kernel, rows, cols), out_shape=pltpu.VME...]
where the time goes in v3:
time: 14 us; the launch traced here: 13.8 us
  Pallas kernels  13.2 us (94%)
  local copies, waits for them, and re-layouts  0.58 us (4%)
    pallas_call x1, Pallas kernels, body(): pl.pallas_call(functools.partial(kernel, rows, cols), out_shape=pltpu.VME...  13.2 us
    unnamed x1, local copies, waits for them, and re-layouts  0.58 us

profile of v3, /device:TPU:0, one launch (start us, length us, event | category | flops | bytes accessed | tf_op | source)
XLA Modules:
  0.0 13.8 jit_solution(3414534885387628591)
XLA Ops:
  0.0 13.2 %shard_map.17 = f32[3,96]{1,0:T(4,128)S(1)} custom-call(f32[3,3,1024]{2,1,0:T(4,128)} %x_hbm.1), custom_call_target="tpu_custom_call" | custom-call | tf_op jit(solution)/shard_map/pallas_call | solution.py:435
  13.3 0.6 %copy.3 = f32[3,96]{1,0:T(4,128)} copy(f32[3,96]{1,0:T(4,128)S(1)} %shard_map.17) | data formatting | bytes 2304

commit v4 on v3

--- a/solution.py
+++ b/solution.py
@@ -55,6 +55,7 @@
     from_plane_sem,
     from_column_sem,
     table_sem,
+    up_sem,
 ):
     n, comps, samples = x_ref.shape
     chunks = samples // LANES
@@ -92,26 +93,42 @@
     def mates(step):
         each(plane - 1, lambda k: step(mate(k + 1)))
 
-    def below(step):
-        for z in range(deep - 1):
-            for core in range(CORES):
-                when(z < my_z, lambda: step(z, core))
+    def compared(z, to):
+        return (z > 0) & ((to == 0) | (to == z + 1) | ((to > 0) & (to < z - 1)))
+
+    hosted = jnp.where(
+        my_z == 0,
+        deep - 1,
+        jnp.where(my_z > 1, 1, 0) + jnp.maximum(deep - 2 - my_z, 0),
+    )
 
     def above(step):
         for z in range(1, deep):
             for core in range(CORES):
                 when(z > my_z, lambda: step(z, core))
 
+    corner = plane - 1, deep - 1
+    at_origin = (my_xy == 0) & (my_z == 0)
+    at_corner = (my_xy == corner[0]) & (my_z == corner[1])
+    at_foot = (my_xy == corner[0]) & (my_z == 0)
+
     barrier = pltpu.get_barrier_semaphore()
 
     def greet(xy, z, core):
         pl.semaphore_signal(barrier, inc=1, device_id=place(xy, z, core), device_id_type=MESH)
+
+    def announce(z, core):
+        pl.semaphore_signal(
+            up_sem, inc=1, device_id=place(my_xy, z, core), device_id_type=MESH
+        )
 
     taken = pltpu.make_async_copy(x_hbm, x_ref, table_sem.at[0])
     taken.start()
     mates(lambda xy: greet(xy, my_z, other))
     above(lambda z, core: greet(my_xy, z, core))
     greet(my_xy, my_z, other)
+    for core in range(CORES):
+        when(at_origin, lambda: greet(*corner, core))
     taken.wait()
 
     for t in range(n):
@@ -125,7 +142,7 @@
     column_blocks[my_z, my_core] = (
         stage[...].reshape(comps, n, chunks, LANES).astype(jnp.bfloat16)
     )
-    pl.semaphore_wait(barrier, CORES * my_z + plane)
+    pl.semaphore_wait(barrier, CORES * my_z + plane + jnp.where(at_corner, CORES, 0))
 
     mine = column_blocks.at[my_z, my_core]
 
@@ -139,6 +156,16 @@
             device_id_type=MESH,
         )
 
+    def to_origin(core):
+        return pltpu.make_async_remote_copy(
+            src_ref=mine,
+            dst_ref=column_blocks.at[deep, my_core],
+            send_sem=column_send_sem.at[deep * CORES + core],
+            recv_sem=column_sem.at[deep * CORES + my_core],
+            device_id=place(0, 0, core),
+            device_id_type=MESH,
+        )
+
     def to_mate(xy):
         return pltpu.make_async_remote_copy(
             src_ref=mine,
@@ -170,20 +197,16 @@
             device_id_type=MESH,
         )
 
-    def send_down(z):
+    def send_to(z):
         to_column(z, my_core).start()
         to_column(z, other).start()
 
-    when(my_z > 0, lambda: send_down(0))
+    when(my_z > 0, lambda: send_to(0))
     mates(lambda xy: to_mate(xy).start())
     to_column(my_z, other).start()
     def gone(z):
         for core in range(CORES):
             to_column(z, core).wait_send()
-
-    def send_next(z):
-        gone(z - 1)
-        send_down(z)
 
 
     for m in range(phases // 2):
@@ -204,6 +227,8 @@
 
     segments = LANES // STEP
     seats_of = segments // 2
+
+    room = 2 * STEP
 
     def stand(g):
         held = range(2 * g, min(2 * g + 2, plane))
@@ -231,11 +256,24 @@
             stood = jnp.concatenate(parts, axis=0).T
             at = slice(g * LANES, (g + 1) * LANES)
             shifts[c * samples : (c + 1) * samples, at] = stood[:samples]
-            tail = comps * samples + c * LANES
-            shifts[tail : tail + LANES, at] = stood[samples:]
+            tail = comps * samples + c * room
+            shifts[tail : tail + room, at] = stood[samples : samples + room]
+        unused = comps * samples + comps * room
+        shifts[unused:, g * LANES : (g + 1) * LANES] = jnp.zeros(
+            (shifts.shape[0] - unused, LANES), jnp.bfloat16
+        )
 
     for z in range(1, deep - 1):
-        when(z < my_z, lambda: send_next(z))
+        for core in range(CORES):
+            when(my_z == z + 1, lambda: announce(z, core))
+    when(my_z > 0, lambda: gone(0))
+    for core in range(CORES):
+        when(at_corner, lambda: to_origin(core).start())
+    for z in range(1, deep - 2):
+        when(my_z > z + 1, lambda: send_to(z))
+    when((my_z > 0) & (my_z < deep - 1), lambda: pl.semaphore_wait(up_sem, CORES))
+    for z in range(2, deep):
+        when(my_z == z - 1, lambda: send_to(z))
     for g in range((plane + 1) // 2):
         stand(g)
 
@@ -263,12 +301,15 @@
     tops = lax.broadcasted_iota(jnp.int32, (SUBS, width), 0)
     place_lane = lax.broadcasted_iota(jnp.int32, (SUBS, 2 * LANES), 1)
     seat = place_lane % STEP
-
-    def compare(z, own):
+    tail_lane = lax.broadcasted_iota(jnp.int32, (2 * SUBS, LANES), 1)
+
+    def compare(z, kind, final=False):
+        own, above_me = kind == "own", kind == "above"
         target = jnp.full((SUBS, width), -1, jnp.int32)
         for core in range(CORES):
             here = (tops >= core * n) & (tops < (core + 1) * n)
-            target = jnp.where(here, column(my_xy, z, core) - core * n + tops, target)
+            seat_of = column(*corner, core) if kind == "corner" else column(my_xy, z, core)
+            target = jnp.where(here, seat_of - core * n + tops, target)
         spot = lane == target
 
         def prepare(c):
@@ -296,6 +337,18 @@
                 parts.append(waves[p % phases // 2, c, :, start : start + size])
             return jnp.concatenate(parts, axis=0)
 
+        def lined_up_tails():
+            parts = []
+            for p in range(0, blocks // 2, 2):
+                joined = None
+                for c in range(comps):
+                    turn = p % phases // 2 - c
+                    start = samples + (p // phases + turn // (phases // 2)) * LANES
+                    piece = waves[turn % (phases // 2), c, :, start : start + LANES]
+                    joined = piece if c == 0 else jnp.where(tail_lane < c * room, joined, piece)
+                parts.append(joined)
+            return jnp.concatenate(parts, axis=0)
+
         def products(g):
             at = slice(2 * g * LANES, 2 * (g + 1) * LANES)
             found = jnp.zeros(((blocks + 2) * SUBS, 2 * LANES), jnp.float32)
@@ -307,16 +360,19 @@
                         shifts[base : base + 2 * LANES, at],
                         preferred_element_type=jnp.float32,
                     )
-            for c in range(comps):
-                base = comps * samples + c * LANES
-                found = found + jnp.dot(
-                    lined_up(c, samples, LANES),
-                    shifts[base : base + LANES, at],
-                    preferred_element_type=jnp.float32,
-                )
-            return found
+            middle = blocks // 2 * SUBS
+            ends = jnp.dot(
+                lined_up_tails(),
+                shifts[comps * samples : comps * samples + LANES, at],
+                preferred_element_type=jnp.float32,
+            )
+            return jnp.concatenate([found[:middle] + ends, found[middle:]], axis=0)
 
         wholes = shifts.shape[1] // (2 * LANES)
+        parted = at_foot & (z == deep - 1)
+        if above_me:
+            for k in range(1, plane):
+                when(parted & (mate(k) == 0), lambda: answer(k).start())
         if own:
             from_above(z, other).wait_recv()
         else:
@@ -340,16 +396,20 @@
             swapped = jnp.maximum(middle, jnp.where(seat == 0, part(blocks), part(0)))
             parts.append(swapped)
             for k, t, part_at, inside in seats(g):
-                if own:
+                if own or (kind == "corner" and k):
                     break
+                into = k if kind == "corner" else jnp.where(parted & (mate(k) == 0), plane, k)
                 best = jnp.max(
                     jnp.where(inside, plain[:, part_at], -jnp.inf), axis=1, keepdims=True
                 )
-                answers[k, t : t + 1] += jnp.sum(
+                answers[into, t : t + 1] += jnp.sum(
                     jnp.where(spot, best, 0.0), axis=0, keepdims=True
                 )
-        if not own:
-            when(z == deep - 1, lambda: each(plane - 1, lambda k: answer(k + 1).start()))
+        if kind == "corner":
+            return
+        if above_me:
+            for k in range(1, plane):
+                when(final & ~(parted & (mate(k) == 0)), lambda: answer(k).start())
         for g in range(wholes):
             for k, t, part_at, inside in seats(g):
                 best = jnp.max(
@@ -372,8 +432,15 @@
                 part_at = slice(s // segments * LANES, (s // segments + 1) * LANES)
                 yield k, t, part_at, (v >= 0) & (v < STEP)
 
-    lax.fori_loop(my_z + 1, deep, lambda z, carry: (compare(z, False), carry)[1], 0)
-    compare(my_z, True)
+    def one_by_one(i, carry):
+        up = jnp.where(i == 0, my_z - 1, my_z + 1 + i)
+        z = jnp.where(my_z == 0, i + 1, jnp.where(my_z > 1, up, my_z + 2 + i))
+        compare(z, "above", i == hosted - 1)
+        return carry
+
+    lax.fori_loop(0, hosted, one_by_one, 0)
+    compare(my_z, "own")
+    when(at_origin, lambda: compare(deep, "corner"))
 
     total[...] = turned_rows[my_z]
 
@@ -390,7 +457,10 @@
 
     for z in range(deep):
         for core in range(CORES):
-            when((z < my_z) | ((z == my_z) & (core != my_core)), lambda: collect(z, core))
+            when(
+                compared(my_z, z) | ((z == my_z) & (core != my_core)),
+                lambda: collect(z, core),
+            )
     total[...] = pltpu.roll(total[...], (SUBS - my_core * n) % SUBS, 0)
     total[...] += answers[0]
 
@@ -405,15 +475,19 @@
         ).wait_recv()
         total[...] += from_plane[xy]
 
-    when(my_z < deep - 1, lambda: mates(hear))
-    out_ref[...] = total[:n, : out_ref.shape[1]]
-
-    when(my_z > 0, lambda: gone(my_z - 1))
+    for z in range(1, deep):
+        when(compared(my_z, z), lambda: gone(z))
     to_column(my_z, other).wait_send()
     mates(lambda xy: to_mate(xy).wait_send())
-    when(my_z < deep - 1, lambda: each(plane - 1, lambda k: answer(k + 1).wait_send()))
-    above(lambda z, core: give_back(z, core).wait_send())
+    when(hosted > 0, lambda: each(plane - 1, lambda k: answer(k + 1).wait_send()))
+    for z in range(1, deep):
+        for core in range(CORES):
+            when(compared(z, my_z), lambda: give_back(z, core).wait_send())
     give_back(my_z, other).wait_send()
+    for core in range(CORES):
+        when(at_corner, lambda: to_origin(core).wait_send())
+    when(hosted > 0, lambda: mates(hear))
+    out_ref[...] = total[:n, : out_ref.shape[1]]
 
 
 def body(templates):
@@ -441,27 +515,28 @@
             pltpu.VMEM(templates.shape, jnp.float32),
             pltpu.VMEM((lines, LANES), jnp.float32),
             pltpu.VMEM((plane, comps, n, chunks, LANES), jnp.bfloat16),
-            pltpu.VMEM((deep, CORES, comps, n, chunks, LANES), jnp.bfloat16),
+            pltpu.VMEM((deep + 1, CORES, comps, n, chunks, LANES), jnp.bfloat16),
             pltpu.VMEM((plane * lines, LANES), jnp.float32),
             pltpu.VMEM((comps, SUBS * chunks, LANES), jnp.float32),
             pltpu.VMEM(
                 (LANES // STEP // 2, comps, 2 * SUBS, samples + 5 * LANES), jnp.bfloat16
             ),
-            pltpu.VMEM((comps * tiles * LANES, spread), jnp.bfloat16),
-            pltpu.VMEM((plane, SUBS, width), jnp.float32),
+            pltpu.VMEM((comps * samples + LANES, spread), jnp.bfloat16),
+            pltpu.VMEM((plane + 1, SUBS, width), jnp.float32),
             pltpu.VMEM((deep, SUBS, width), jnp.float32),
             pltpu.VMEM((plane, SUBS, width), jnp.float32),
             pltpu.VMEM((deep, CORES, SUBS, width), jnp.float32),
             pltpu.VMEM((SUBS, width), jnp.float32),
             dma((plane,)),
-            dma((deep * CORES,)),
-            dma((deep * CORES,)),
+            dma(((deep + 1) * CORES,)),
+            dma(((deep + 1) * CORES,)),
             dma((plane,)),
             dma((plane,)),
             dma((deep * CORES,)),
             dma((plane,)),
             dma((deep * CORES,)),
             dma((1,)),
+            pltpu.SemaphoreType.REGULAR,
         ],
         compiler_params=pltpu.CompilerParams(collective_id=0, has_side_effects=True),
     )(templates)

time: 14 us -> 13.4 us (0.957)
  Pallas kernels: 13.2 us -> 12.6 us
    pallas_call x1, Pallas kernels: 13.2 us -> 12.6 us  [body(): pl.pallas_call(functools.partial(kernel, rows, cols), out_shape=pltpu.VME...]
where the time goes in v4:
time: 13.4 us; the launch traced here: 13.2 us
  Pallas kernels  12.6 us (94%)
  local copies, waits for them, and re-layouts  0.58 us (4%)
    pallas_call x1, Pallas kernels, body(): pl.pallas_call(functools.partial(kernel, rows, cols), out_shape=pltpu.VME...  12.6 us
    unnamed x1, local copies, waits for them, and re-layouts  0.58 us

profile of v4, /device:TPU:0, one launch (start us, length us, event | category | flops | bytes accessed | tf_op | source)
XLA Modules:
  0.0 13.2 jit_solution(7860695507593604740)
XLA Ops:
  0.0 12.6 %shard_map.17 = f32[3,96]{1,0:T(4,128)S(1)} custom-call(f32[3,3,1024]{2,1,0:T(4,128)} %x_hbm.1), custom_call_target="tpu_custom_call" | custom-call | tf_op jit(solution)/shard_map/pallas_call | solution.py:509
  12.6 0.6 %copy.3 = f32[3,96]{1,0:T(4,128)} copy(f32[3,96]{1,0:T(4,128)S(1)} %shard_map.17) | data formatting | bytes 2304

commit v5 on v4

--- a/solution.py
+++ b/solution.py
@@ -187,6 +187,17 @@
             device_id_type=MESH,
         )
 
+    def hand_over():
+        block = column_blocks.at[deep - 1, other]
+        return pltpu.make_async_remote_copy(
+            src_ref=block,
+            dst_ref=block,
+            send_sem=column_send_sem.at[(deep - 1) * CORES],
+            recv_sem=column_sem.at[(deep - 1) * CORES + other],
+            device_id=place(my_xy, my_z, other),
+            device_id_type=MESH,
+        )
+
     def from_mate(xy):
         return pltpu.make_async_remote_copy(
             src_ref=mine,
@@ -198,15 +209,21 @@
         )
 
     def send_to(z):
-        to_column(z, my_core).start()
+        if z == 0:
+            when(~at_corner, lambda: to_column(z, my_core).start())
+        else:
+            to_column(z, my_core).start()
         to_column(z, other).start()
 
     when(my_z > 0, lambda: send_to(0))
     mates(lambda xy: to_mate(xy).start())
     to_column(my_z, other).start()
     def gone(z):
-        for core in range(CORES):
-            to_column(z, core).wait_send()
+        if z == 0:
+            when(~at_corner, lambda: to_column(z, my_core).wait_send())
+        else:
+            to_column(z, my_core).wait_send()
+        to_column(z, other).wait_send()
 
 
     for m in range(phases // 2):
@@ -376,8 +393,10 @@
         if own:
             from_above(z, other).wait_recv()
         else:
-            for core in range(CORES):
-                from_above(z, core).wait_recv()
+            from_above(z, other).wait_recv()
+            if above_me:
+                when(parted, lambda: hand_over().start())
+            from_above(z, my_core).wait_recv()
         for c in range(comps):
             prepare(c)
 
@@ -438,8 +457,10 @@
         compare(z, "above", i == hosted - 1)
         return carry
 
+    late_own = (my_z == 0) & (my_xy > 0)
+    when(~late_own, lambda: compare(my_z, "own"))
     lax.fori_loop(0, hosted, one_by_one, 0)
-    compare(my_z, "own")
+    when(late_own, lambda: compare(my_z, "own"))
     when(at_origin, lambda: compare(deep, "corner"))
 
     total[...] = turned_rows[my_z]
@@ -486,6 +507,7 @@
     give_back(my_z, other).wait_send()
     for core in range(CORES):
         when(at_corner, lambda: to_origin(core).wait_send())
+    when(at_foot, lambda: hand_over().wait_send())
     when(hosted > 0, lambda: mates(hear))
     out_ref[...] = total[:n, : out_ref.shape[1]]
 

time: 13.4 us -> 13.2 us (0.985)
    pallas_call x1, Pallas kernels: 12.6 us -> 12.5 us  [body(): pl.pallas_call(functools.partial(kernel, rows, cols), out_shape=pltpu.VME...]
where the time goes in v5:
time: 13.2 us; the launch traced here: 13.1 us
  Pallas kernels  12.5 us (95%)
  local copies, waits for them, and re-layouts  0.58 us (4%)
    pallas_call x1, Pallas kernels, body(): pl.pallas_call(functools.partial(kernel, rows, cols), out_shape=pltpu.VME...  12.5 us
    unnamed x1, local copies, waits for them, and re-layouts  0.58 us

profile of v5, /device:TPU:0, one launch (start us, length us, event | category | flops | bytes accessed | tf_op | source)
XLA Modules:
  0.0 13.1 jit_solution(2933866489048989450)
XLA Ops:
  0.0 12.5 %shard_map.17 = f32[3,96]{1,0:T(4,128)S(1)} custom-call(f32[3,3,1024]{2,1,0:T(4,128)} %x_hbm.1), custom_call_target="tpu_custom_call" | custom-call | tf_op jit(solution)/shard_map/pallas_call | solution.py:531
  12.5 0.6 %copy.3 = f32[3,96]{1,0:T(4,128)} copy(f32[3,96]{1,0:T(4,128)S(1)} %shard_map.17) | data formatting | bytes 2304

commit v6 on v5

--- a/solution.py
+++ b/solution.py
@@ -56,6 +56,7 @@
     from_column_sem,
     table_sem,
     up_sem,
+    mate_sem,
 ):
     n, comps, samples = x_ref.shape
     chunks = samples // LANES
@@ -124,11 +125,28 @@
 
     taken = pltpu.make_async_copy(x_hbm, x_ref, table_sem.at[0])
     taken.start()
-    mates(lambda xy: greet(xy, my_z, other))
+    hub = plane - 1
+    at_hub = my_xy == hub
+    for core in range(CORES):
+        when((my_z > 0) & ~at_hub, lambda: greet(hub, my_z, core))
+    when(my_z == 0, lambda: mates(lambda xy: greet(xy, my_z, other)))
     above(lambda z, core: greet(my_xy, z, core))
     greet(my_xy, my_z, other)
     for core in range(CORES):
         when(at_origin, lambda: greet(*corner, core))
+    waited = CORES * my_z + 1 + jnp.where(at_hub, CORES * (plane - 1), 0)
+    waited = waited + jnp.where(at_corner, CORES, 0)
+    when(my_z > 0, lambda: pl.semaphore_wait(barrier, waited))
+
+    def admit(xy):
+        pl.semaphore_signal(
+            mate_sem, inc=1, device_id=place(xy, my_z, other), device_id_type=MESH
+        )
+
+    when((my_z > 0) & at_hub, lambda: mates(admit))
+    for z in range(1, deep - 1):
+        for core in range(CORES):
+            when(my_z == z + 1, lambda: announce(z, core))
     taken.wait()
 
     for t in range(n):
@@ -142,7 +160,8 @@
     column_blocks[my_z, my_core] = (
         stage[...].reshape(comps, n, chunks, LANES).astype(jnp.bfloat16)
     )
-    pl.semaphore_wait(barrier, CORES * my_z + plane + jnp.where(at_corner, CORES, 0))
+
+    when(my_z == 0, lambda: pl.semaphore_wait(barrier, plane))
 
     mine = column_blocks.at[my_z, my_core]
 
@@ -216,8 +235,11 @@
         to_column(z, other).start()
 
     when(my_z > 0, lambda: send_to(0))
+    for core in range(CORES):
+        when(at_corner, lambda: to_origin(core).start())
+    to_column(my_z, other).start()
+    when((my_z > 0) & ~at_hub, lambda: pl.semaphore_wait(mate_sem, 1))
     mates(lambda xy: to_mate(xy).start())
-    to_column(my_z, other).start()
     def gone(z):
         if z == 0:
             when(~at_corner, lambda: to_column(z, my_core).wait_send())
@@ -280,12 +302,7 @@
             (shifts.shape[0] - unused, LANES), jnp.bfloat16
         )
 
-    for z in range(1, deep - 1):
-        for core in range(CORES):
-            when(my_z == z + 1, lambda: announce(z, core))
     when(my_z > 0, lambda: gone(0))
-    for core in range(CORES):
-        when(at_corner, lambda: to_origin(core).start())
     for z in range(1, deep - 2):
         when(my_z > z + 1, lambda: send_to(z))
     when((my_z > 0) & (my_z < deep - 1), lambda: pl.semaphore_wait(up_sem, CORES))
@@ -496,6 +513,9 @@
         ).wait_recv()
         total[...] += from_plane[xy]
 
+    when(hosted > 0, lambda: mates(hear))
+    out_ref[...] = total[:n, : out_ref.shape[1]]
+
     for z in range(1, deep):
         when(compared(my_z, z), lambda: gone(z))
     to_column(my_z, other).wait_send()
@@ -508,8 +528,6 @@
     for core in range(CORES):
         when(at_corner, lambda: to_origin(core).wait_send())
     when(at_foot, lambda: hand_over().wait_send())
-    when(hosted > 0, lambda: mates(hear))
-    out_ref[...] = total[:n, : out_ref.shape[1]]
 
 
 def body(templates):
@@ -559,6 +577,7 @@
             dma((deep * CORES,)),
             dma((1,)),
             pltpu.SemaphoreType.REGULAR,
+            pltpu.SemaphoreType.REGULAR,
         ],
         compiler_params=pltpu.CompilerParams(collective_id=0, has_side_effects=True),
     )(templates)

time: 13.2 us -> 13.1 us (level)
  no operation moved by 1% of the time
where the time goes in v6:
time: 13.1 us; the launch traced here: 13 us
  Pallas kernels  12.4 us (95%)
  local copies, waits for them, and re-layouts  0.58 us (4%)
    pallas_call x1, Pallas kernels, body(): pl.pallas_call(functools.partial(kernel, rows, cols), out_shape=pltpu.VME...  12.4 us
    unnamed x1, local copies, waits for them, and re-layouts  0.58 us

profile of v6, /device:TPU:0, one launch (start us, length us, event | category | flops | bytes accessed | tf_op | source)
XLA Modules:
  0.0 13.0 jit_solution(7104594654116613686)
XLA Ops:
  0.0 12.4 %shard_map.17 = f32[3,96]{1,0:T(4,128)S(1)} custom-call(f32[3,3,1024]{2,1,0:T(4,128)} %x_hbm.1), custom_call_target="tpu_custom_call" | custom-call | tf_op jit(solution)/shard_map/pallas_call | solution.py:549
  12.4 0.6 %copy.3 = f32[3,96]{1,0:T(4,128)} copy(f32[3,96]{1,0:T(4,128)S(1)} %shard_map.17) | data formatting | bytes 2304

commit v7 on v6

--- a/solution.py
+++ b/solution.py
@@ -385,15 +385,11 @@
 
         def products(g):
             at = slice(2 * g * LANES, 2 * (g + 1) * LANES)
-            found = jnp.zeros(((blocks + 2) * SUBS, 2 * LANES), jnp.float32)
-            for c in range(comps):
-                for start in range(0, samples, 2 * LANES):
-                    base = c * samples + start
-                    found = found + jnp.dot(
-                        lined_up(c, start, 2 * LANES),
-                        shifts[base : base + 2 * LANES, at],
-                        preferred_element_type=jnp.float32,
-                    )
+            found = jnp.dot(
+                jnp.concatenate([lined_up(c, 0, samples) for c in range(comps)], axis=1),
+                shifts[: comps * samples, at],
+                preferred_element_type=jnp.float32,
+            )
             middle = blocks // 2 * SUBS
             ends = jnp.dot(
                 lined_up_tails(),

time: 13.1 us -> 13.1 us (level)
  no operation moved by 1% of the time
where the time goes in v7:
time: 13.1 us; the launch traced here: 13 us
  Pallas kernels  12.4 us (95%)
  local copies, waits for them, and re-layouts  0.58 us (4%)
    pallas_call x1, Pallas kernels, body(): pl.pallas_call(functools.partial(kernel, rows, cols), out_shape=pltpu.VME...  12.4 us
    unnamed x1, local copies, waits for them, and re-layouts  0.58 us

profile of v7, /device:TPU:0, one launch (start us, length us, event | category | flops | bytes accessed | tf_op | source)
XLA Modules:
  0.0 13.0 jit_solution(16332850795059446766)
XLA Ops:
  0.0 12.4 %shard_map.17 = f32[3,96]{1,0:T(4,128)S(1)} custom-call(f32[3,3,1024]{2,1,0:T(4,128)} %x_hbm.1), custom_call_target="tpu_custom_call" | custom-call | tf_op jit(solution)/shard_map/pallas_call | solution.py:545
  12.4 0.6 %copy.3 = f32[3,96]{1,0:T(4,128)} copy(f32[3,96]{1,0:T(4,128)S(1)} %shard_map.17) | data formatting | bytes 2304

commit v8 on v7

--- a/solution.py
+++ b/solution.py
@@ -366,7 +366,7 @@
 
         def lined_up(c, at, size):
             parts = []
-            for p in range(0, blocks + 2, 2):
+            for p in range(0, blocks if kind == "corner" else blocks + 2, 2):
                 start = at + p // phases * LANES
                 parts.append(waves[p % phases // 2, c, :, start : start + size])
             return jnp.concatenate(parts, axis=0)
@@ -425,8 +425,10 @@
             for p in range(2, blocks):
                 middle = jnp.maximum(middle, part(p))
             plain = jnp.maximum(middle, part(0))
-            swapped = jnp.maximum(middle, jnp.where(seat == 0, part(blocks), part(0)))
-            parts.append(swapped)
+            if kind != "corner":
+                parts.append(
+                    jnp.maximum(middle, jnp.where(seat == 0, part(blocks), part(0)))
+                )
             for k, t, part_at, inside in seats(g):
                 if own or (kind == "corner" and k):
                     break

time: 13.1 us -> 13.1 us (level)
  no operation moved by 1% of the time
where the time goes in v8:
time: 13.1 us; the launch traced here: 13 us
  Pallas kernels  12.4 us (95%)
  local copies, waits for them, and re-layouts  0.58 us (4%)
    pallas_call x1, Pallas kernels, body(): pl.pallas_call(functools.partial(kernel, rows, cols), out_shape=pltpu.VME...  12.4 us
    unnamed x1, local copies, waits for them, and re-layouts  0.58 us

profile of v8, /device:TPU:0, one launch (start us, length us, event | category | flops | bytes accessed | tf_op | source)
XLA Modules:
  0.0 13.0 jit_solution(1247049653927385769)
XLA Ops:
  0.0 12.4 %shard_map.17 = f32[3,96]{1,0:T(4,128)S(1)} custom-call(f32[3,3,1024]{2,1,0:T(4,128)} %x_hbm.1), custom_call_target="tpu_custom_call" | custom-call | tf_op jit(solution)/shard_map/pallas_call | solution.py:547
  12.4 0.6 %copy.3 = f32[3,96]{1,0:T(4,128)} copy(f32[3,96]{1,0:T(4,128)S(1)} %shard_map.17) | data formatting | bytes 2304
